TPU v7x, 32 devices: a whole 2x2x4 slice. The times are simulated.
32 devices in a mesh: shard: 8 (over y, x, core), dp: 4 (over z).
Axes of the slice: x: 2, y: 2, z: 4, core: 2. Of those that a mesh axis runs over, the one named last changes fastest.
Arguments:
- grad: float32 [288, 128, 4096], P('shard', 'dp'), may hold values from -252 to 252
- param: bfloat16 [288, 128, 4096], P('shard', 'dp'), may hold values from -0.119628906 to 0.119628906
- row_state: float32 [288, 128], P('shard', 'dp'), may hold values from 0.3 to 27
- col_state: float32 [3, 4096], replicated, may hold values from 0.002 to 400
- block_start: int32 [8], replicated, may hold values from 0 to 143, as said below
- block_matrix: int32 [144], replicated, may hold values from 0 to 2, as said below
- step: int32 [1], replicated, may hold values from 2 to 11
Outputs:
- new_params: bfloat16 [18432, 4096], P(None, 'shard')
- new_row_state: float32 [288, 128], P('shard', 'dp')
- new_col_state: float32 [3, 4096], replicated
Inputs may be any that keep to these rules, and one draw needn't show every extreme that they name: block_start rises from 0 at index 0; every shard index owns between 1 and 36 consecutive global blocks, held in its first slots, and some index owns exactly 36; slots past a device's owned count hold values that no output reads. `block_matrix`: ids 0 and 1 each label 4096 / 128 blocks and id 2 labels 10240 / 128 blocks, in any order.
All inputs are finite; a program needn't handle non-finite values.
Results may differ from a plain program's by a relative error of at most 0.0004.
Values may be sent and summed in bfloat16 or wider, within the bound.
A program may use at most 192 MiB of HBM per device.

v0:
```python
import jax
import jax.numpy as jnp
from jax import lax
from jax.sharding import PartitionSpec as P

D = 4096
FF = 10240


def scale_grad(grad, safe_rows, matrix_pick, new_cols, row_avg):
    slot_cols = jnp.dot(matrix_pick, new_cols, precision=lax.Precision.HIGHEST)
    slot_avg = jnp.dot(matrix_pick, row_avg, precision=lax.Precision.HIGHEST)
    return grad / jnp.sqrt(safe_rows[:, :, None] * slot_cols[:, None, :] / slot_avg[:, None, None])


def body(grad, param, row_state, col_state, block_start, block_matrix, step):
    slot_count = grad.shape[0]
    total_blocks = block_matrix.shape[0]
    shard_index = lax.axis_index("shard")
    block_ends = jnp.concatenate([block_start[1:], jnp.full((1,), total_blocks, jnp.int32)])
    first_block = lax.dynamic_index_in_dim(block_start, shard_index, keepdims=False)
    owned_count = lax.dynamic_index_in_dim(block_ends, shard_index, keepdims=False) - first_block
    slot_ids = jnp.arange(slot_count, dtype=jnp.int32)
    live_slot = slot_ids < owned_count
    block_ids = first_block + slot_ids
    block_table = block_ids[:, None] == jnp.arange(total_blocks, dtype=jnp.int32)[None, :]
    matrix_ids = jnp.sum(jnp.where(block_table, block_matrix[None, :], 0), axis=1)
    matrix_ids = jnp.where(live_slot, matrix_ids, 0)
    matrix_pick = (matrix_ids[:, None] == jnp.arange(3, dtype=jnp.int32)[None, :]).astype(
        jnp.float32
    )
    member = matrix_pick * live_slot[:, None].astype(jnp.float32)
    row_count = jnp.array([D, D, FF], jnp.float32)
    step_value = step[0].astype(jnp.float32)
    decay_rate = 1.0 - step_value ** (-0.8)
    learn_rate = 1.0 / jnp.sqrt(jnp.maximum(step_value, 10000.0))
    squares = grad * grad
    new_rows = jnp.where(
        live_slot[:, None],
        decay_rate * row_state + (1.0 - decay_rate) * jnp.sum(squares, axis=2) / D,
        0.0,
    )
    safe_rows = jnp.where(live_slot[:, None], new_rows, 1.0)
    col_part = jnp.einsum(
        "sm,sd->md", member, jnp.sum(squares, axis=1), precision=lax.Precision.HIGHEST
    )
    row_part = jnp.dot(jnp.sum(new_rows, axis=1), member, precision=lax.Precision.HIGHEST)
    col_total, row_total = lax.psum((col_part, row_part), ("shard", "dp"))
    new_cols = decay_rate * col_state + (1.0 - decay_rate) * col_total / row_count[:, None]
    row_avg = row_total / row_count
    scaled = scale_grad(grad, safe_rows, matrix_pick, new_cols, row_avg)
    square_part = jnp.dot(
        jnp.sum(scaled * scaled, axis=(1, 2)), member, precision=lax.Precision.HIGHEST
    )
    square_total = lax.psum(square_part, ("shard", "dp"))
    clip_factor = jnp.maximum(1.0, jnp.sqrt(square_total / (row_count * D)))
    slot_clip = jnp.dot(matrix_pick, clip_factor, precision=lax.Precision.HIGHEST)
    updated = jnp.where(
        live_slot[:, None, None],
        param.astype(jnp.float32) - learn_rate * scaled / slot_clip[:, None, None],
        0.0,
    ).astype(jnp.bfloat16)
    column_rows = lax.all_to_all(updated, "shard", split_axis=2, concat_axis=0, tiled=True)
    spread = lax.all_gather(column_rows, "dp", axis=1, tiled=True)
    block_index = jnp.arange(total_blocks, dtype=jnp.int32)
    block_owner = (
        jnp.sum((block_start[None, :] <= block_index[:, None]).astype(jnp.int32), axis=1) - 1
    )
    slot_of = block_owner * slot_count + block_index - jnp.take(block_start, block_owner)
    new_params = jnp.take(spread, slot_of, axis=0).reshape(
        total_blocks * spread.shape[1], spread.shape[2]
    )
    return (new_params, new_rows, new_cols)


def solution(mesh):
    return jax.shard_map(
        body,
        mesh=mesh,
        in_specs=(
            P("shard", "dp", None),
            P("shard", "dp", None),
            P("shard", "dp"),
            P(),
            P(),
            P(),
            P(),
        ),
        out_specs=(P(None, "shard"), P("shard", "dp"), P()),
        check_vma=False,
    )
```

profile of v0, /device:TPU:0, one launch (start us, length us, event | category | flops | bytes accessed | tf_op | source)
XLA Modules:
  0.0 1281.9 jit_solution(16187082374226988263)
XLA Ops:
  7.2 0.0 all-gather.2.cloned.1.call-start
  7.2 0.7 slice.3
  7.9 1.7 fusion.30
  9.6 0.1 pad_add_fusion
  9.7 0.6 dynamic_slice.7
  10.3 0.6 iota_add_fusion
  12.2 0.9 select_reduce_fusion
  13.8 10.8 multiply_reduce_fusion.1
  24.5 0.8 copy.31
  25.4 0.1 broadcast_select_fusion
  25.5 0.1 reduce_sum.58
  25.6 0.2 convolution_bitcast_fusion.1
  25.8 0.6 fusion.2
  26.4 0.0 copy-start.1
  26.4 0.0 copy-start.3
  26.4 52.1 %copy.34 = f32[36,32,4096]{0,1,2:T(8,128)} copy(f32[36,32,4096]{2,1,0:T(8,128)} %param.8) | data formatting | bytes 37748736 | tf_op args[0]
  78.5 42.6 %all-reduce = (f32[3]{0:T(128)S(1)}, f32[3,4096]{1,0:T(4,128)S(1)}) all-reduce(f32[3]{0:T(128)S(1)} %convolution_bitcast_fusion.1, f32[3,4096]{1,0:T(4,128)S(1)} %fusion.2), channel_id=1, replica_groups=mesh['shard'=8,'dp'=4] {'shard','dp'}, use_global_device_ids=true, to_apply=%region_6.7 | all-reduce | flops 12291 | bytes 98328 | tf_op jit(solution)/shard_map/psum | solution.py:48
  121.1 0.0 copy-done.1
  121.1 0.0 copy-done.3
  121.1 0.1 multiply_add_fusion
  121.2 0.0 copy-start
  121.2 1.8 fusion.4
  123.0 0.2 convolution_bitcast_fusion.3
  123.2 0.1 copy.32
  123.3 21.6 %multiply_reduce_fusion = f32[36]{0:T(128)S(1)} fusion(f32[36,32,4096]{0,1,2:T(8,128)} %copy.34, f32[36]{0:T(128)S(1)} %convolution_bitcast_fusion.3, f32[36,4096]{0,1:T(8,128)S(1)} %fusion.4, f32[36,32]{0,1:T(8,128)S(1)} %copy.32), kind=kLoop, calls=%fused_computation.2 | loop fusion | flops 23592924 | bytes 19469088 | tf_op jit(solution)/shard_map/reduce_sum | solution.py:53
  144.9 0.0 copy-start.4
  144.9 0.2 convolution_bitcast_fusion
  145.1 40.2 %psum.23 = f32[3]{0:T(128)S(1)} all-reduce(f32[3]{0:T(128)S(1)} %convolution_bitcast_fusion), channel_id=1, replica_groups=mesh['shard'=8,'dp'=4] {'shard','dp'}, use_global_device_ids=true, to_apply=%region_8.9 | all-reduce | flops 3 | bytes 24 | tf_op jit(solution)/shard_map/psum | solution.py:55
  185.4 50.7 %copy.30 = bf16[36,32,4096]{0,1,2:T(8,128)(2,1)} copy(bf16[36,32,4096]{2,1,0:T(8,128)(2,1)} %param.9) | data formatting | bytes 18874368 | tf_op args[1]
  236.1 0.0 copy-done
  236.1 0.0 copy-done.4
  236.1 0.2 convolution_bitcast_fusion.2
  236.2 43.2 %fusion.31 = bf16[4096,32,36]{2,1,0:T(8,128)(2,1)} fusion(f32[36]{0:T(128)S(1)} %convolution_bitcast_fusion.2, f32[36,32,4096]{0,1,2:T(8,128)} %copy.34, f32[36]{0:T(128)S(1)} %convolution_bitcast_fusion.3, f32[36,4096]{0,1:T(8,128)S(1)} %fusion.4, f32[36,32]{0,1:T(8,128)S(1)} %copy.32, f32[]{:T(128)} %bitcast.14, bf16[36,32,4096]{0,1,2:T(8,128)(2,1)} %copy.30, ...), kind=kLoop, calls=%fused_computation.74 | loop fusion | flops 42467328 | bytes 38343496
  279.5 88.9 %reshape.180 = bf16[8,2,294912]{2,1,0:T(2,128)(2,1)} reshape(bf16[4096,32,36]{2,1,0:T(8,128)(2,1)} %fusion.31) | data formatting | bytes 18874368
  368.4 111.2 %all_to_all.18 = bf16[8,2,294912]{2,1,0:T(2,128)(2,1)} all-to-all(bf16[8,2,294912]{2,1,0:T(2,128)(2,1)} %reshape.180), channel_id=1, replica_groups=mesh['shard'=8,'dp'=4] {'shard'}, dimensions={0} | all-to-all | bytes 18874368 | tf_op jit(solution)/shard_map/all_to_all | solution.py:63
  479.6 0.0 copy-start.2
  479.6 94.1 %reshape.181 = bf16[4096,32,36]{2,1,0:T(8,128)(2,1)} reshape(bf16[8,2,294912]{2,1,0:T(2,128)(2,1)} %all_to_all.18) | data formatting | bytes 18874368
  573.7 38.9 %copy.36 = bf16[8,36,32,512]{3,2,1,0:T(8,128)(2,1)} copy(bf16[8,36,32,512]{1,2,3,0:T(8,128)(2,1)} %bitcast.51) | data formatting | bytes 18874368 | tf_op jit(solution)/shard_map/all_to_all | solution.py:63
  612.6 0.0 all-gather.2.cloned.1.call-update
  612.7 0.7 copy.37
  613.4 0.0 copy-done.2
  613.4 0.1 convert_reduce_fusion
  613.5 4.4 compare_select_fusion.2
  617.9 0.6 compare_and_fusion
  618.6 0.1 broadcast_bitcast_fusion
  618.7 623.5 %all-gather.2.cloned.1.call-done = bf16[288,128,512]{2,1,0:T(8,128)(2,1)} async-done(((bf16[288,32,512]{2,1,0:T(8,128)(2,1)}), bf16[288,128,512]{2,1,0:T(8,128)(2,1)}) %all-gather.2.cloned.1.call-update) | async-done | bytes 37748752 | tf_op jit(solution)/shard_map/all_gather | solution.py:64
  1242.2 15.5 %gather_fusion = bf16[144,128,512]{2,1,0:T(8,128)(2,1)} fusion(bf16[288,128,512]{2,1,0:T(8,128)(2,1)} %all-gather.2.cloned.1.call-done, s32[1024]{0:T(1024)S(1)} %pad_clamp_fusion), kind=kCustom, calls=%fused_computation | custom fusion | bytes 37749312 | tf_op jit(solution)/shard_map/jit(_take)/gather | solution.py:70
  1257.8 17.3 %bitcast_select_fusion = bf16[18432,512]{1,0:T(8,128)(2,1)} fusion(bf16[144,128,512]{2,1,0:T(8,128)(2,1)} %gather_fusion, pred[18432]{0:T(1024)(128)(4,1)S(1)} %broadcast_bitcast_fusion), kind=kLoop, calls=%fused_computation.4 | loop fusion | flops 9437184 | bytes 37767168 | tf_op jit(solution)/shard_map/jit(_take)/select_n | solution.py:70
  (6 shorter events, 0.1 us)
Async XLA Ops:
  7.2 1235.1 %all-gather.2.cloned.1.call-start = ((), (), s32[]{:S(2)}) async-start(), calls=%async_computation.1 | async-start | bytes 47185920 | tf_op jit(solution)/shard_map/all_gather | solution.py:64
  26.4 94.7 %copy-start.1 = (f32[3,4096]{1,0:T(4,128)S(1)}, f32[3,4096]{1,0:T(4,128)}, u32[]{:S(2)}) copy-start(f32[3,4096]{1,0:T(4,128)} %param.11) | copy-start | bytes 147460
  26.4 94.7 %copy-start.3 = (f32[3]{0:T(128)S(1)}, f32[3]{0:T(128)}, u32[]{:S(2)}) copy-start(f32[3]{0:T(128)} %constant.78) | copy-start | bytes 40
  121.2 114.9 %copy-start = (f32[3,4096]{1,0:T(4,128)}, f32[3,4096]{1,0:T(4,128)S(1)}, u32[]{:S(2)}) copy-start(f32[3,4096]{1,0:T(4,128)S(1)} %multiply_add_fusion) | copy-start | bytes 147460
  144.9 91.2 %copy-start.4 = (f32[3]{0:T(128)S(1)}, f32[3]{0:T(128)}, u32[]{:S(2)}) copy-start(f32[3]{0:T(128)} %constant.81) | copy-start | bytes 40
  479.6 133.7 %copy-start.2 = (s32[8]{0:T(128)S(1)}, s32[8]{0:T(128)}, u32[]{:S(2)}) copy-start(s32[8]{0:T(128)} %param.12) | copy-start | bytes 100
Sparse Core Ops, SparseCore 0:
  612.8 629.3 all-gather.1
where the time goes:
time: 1280 us
  waiting for transfers between devices  624 us (49%)
  local copies, waits for them, and re-layouts  345 us (27%)
  blocking collectives  194 us (15%)
  other arithmetic  100 us (8%)
  between operations  16.2 us (1%)
    all_gather x1, waiting for transfers between devices, body(): spread = lax.all_gather(column_rows, 'dp', axis=1, tiled=True)  624 us
    unnamed x16, local copies, waits for them, and re-layouts  287 us
    all_to_all x1, blocking collectives, body(): lax.all_to_all(updated, 'shard', split_axis=2, concat_axis=0, tiled=True)  111 us
    unnamed x1, other arithmetic  43.2 us
    psum x1, blocking collectives, body(): col_total, row_total = lax.psum((col_part, row_part), ('shard', 'dp'))  42.6 us
    psum x1, blocking collectives, body(): square_total = lax.psum(square_part, ('shard', 'dp'))  40.2 us
    all_to_all x1, local copies, waits for them, and re-layouts, body(): lax.all_to_all(updated, 'shard', split_axis=2, concat_axis=0, tiled=True)  38.9 us
  transfers between devices with their start and end apart: 1, of which 1 were waited for; matrix products, arithmetic and copies ran while one was open for 0% of the time, Pallas kernels for 0%

commit v1 on v0

v1 whole, which is shorter than its diff:
```python
import functools

import jax
import jax.numpy as jnp
from jax import lax
from jax.experimental import pallas as pl
from jax.experimental.pallas import tpu as pltpu
from jax.sharding import PartitionSpec as P

D = 4096
FF = 10240
MATS = 3
CHUNK = 8


def slots_per_step(slot_count):
    return max(n for n in range(1, 5) if slot_count % n == 0)


def sums_kernel(group, mats, ints_ref, floats_ref, grad_ref, state_ref, rows_ref, sums_ref, cols_acc, weighted_acc, rows_acc):
    step = pl.program_id(0)
    owned = ints_ref[0]
    beta = floats_ref[0]
    gain = floats_ref[1]
    height, width = grad_ref.shape[1], grad_ref.shape[2]

    @pl.when(step == 0)
    def _():
        cols_acc[...] = jnp.zeros_like(cols_acc)
        weighted_acc[...] = jnp.zeros_like(weighted_acc)
        rows_acc[...] = jnp.zeros_like(rows_acc)

    for j in range(group):
        slot = step * group + j

        @pl.when(slot >= owned)
        def _():
            rows_ref[j] = jnp.zeros_like(rows_ref[j])

        @pl.when(slot < owned)
        def _():
            m = ints_ref[2 + slot]
            squares = grad_ref[j] * grad_ref[j]
            rows = beta * state_ref[j] + gain * jnp.sum(squares, axis=1, keepdims=True)
            rows_ref[j] = rows
            tall = (height // 8, 8, width)
            cols_acc[m] += jnp.sum(squares.reshape(tall), axis=0)
            weighted_acc[m] += jnp.sum((squares * (1.0 / rows)).reshape(tall), axis=0)
            rows_acc[m] += jnp.sum(jnp.broadcast_to(rows, (height, 128)).reshape(height // 8, 8, 128), axis=0)

    @pl.when(step == pl.num_programs(0) - 1)
    def _():
        sums_ref[...] = jnp.zeros_like(sums_ref)
        for m in range(mats):
            sums_ref[m : m + 1, :] = jnp.sum(cols_acc[m], axis=0, keepdims=True)
            sums_ref[mats + m : mats + m + 1, :] = jnp.sum(weighted_acc[m], axis=0, keepdims=True)
            sums_ref[2 * mats : 2 * mats + 1, m * 128 : m * 128 + 128] = jnp.sum(rows_acc[m], axis=0, keepdims=True)


def update_kernel(group, mats, parts, row_counts, ints_ref, floats_ref, grad_ref, param_ref, rows_ref, total_ref, state_ref, *refs):
    chunk_refs, (cols_ref, factor) = refs[:-2], refs[-2:]
    step = pl.program_id(0)
    owned, last = ints_ref[0], ints_ref[1]
    beta, rest, rate = floats_ref[0], floats_ref[2], floats_ref[3]
    height, width = grad_ref.shape[1], grad_ref.shape[2]
    cut = width // parts

    @pl.when(step == 0)
    def _():
        for m in range(mats):
            count = row_counts[m]
            cols = beta * state_ref[m : m + 1, :] + rest * (total_ref[m : m + 1, :] / count)
            cols_ref[m : m + 1, :] = cols
            average = total_ref[2 * mats : 2 * mats + 1, m * 128 : m * 128 + 1] / count
            weighted = total_ref[mats + m : mats + m + 1, :]
            square = average * jnp.sum(weighted / cols, axis=1, keepdims=True)
            clip = jnp.maximum(1.0, jnp.sqrt(square / (count * width)))
            factor[m] = lax.rsqrt(cols) * (jnp.sqrt(average) * rate / clip)

    @pl.when(step <= last)
    def _():
        for j in range(group):
            slot = step * group + j

            @pl.when(slot < owned)
            def _():
                m = ints_ref[2 + slot]
                scale = lax.rsqrt(rows_ref[j])
                for k, chunk_ref in enumerate(chunk_refs):
                    at = slice(k * CHUNK, (k + 1) * CHUNK)
                    for n in range(parts):
                        span = slice(n * cut, (n + 1) * cut)
                        new = param_ref[j, at, span].astype(jnp.float32) - grad_ref[j, at, span] * scale[at] * factor[m, :, span]
                        chunk_ref[n, j] = new.astype(chunk_ref.dtype)


def pick_kernel(slot_ref, in_ref, out_ref):
    def move(b, carry):
        out_ref[b] = in_ref[slot_ref[b]]
        return carry

    lax.fori_loop(0, out_ref.shape[0], move, 0, unroll=8)


def place_kernel(in_ref, *refs):
    refs[-1][:, :, 0] = in_ref[...]


def body(parts, grad, param, row_state, col_state, block_start, block_matrix, step):
    slot_count, height, width = grad.shape
    mats = col_state.shape[0]
    total_blocks = block_matrix.shape[0]
    group = slots_per_step(slot_count)
    steps = slot_count // group
    chunks = height // CHUNK
    cut = width // parts
    row_counts = (float(D), float(D), float(FF))

    shard_index = lax.axis_index("shard")
    block_ends = jnp.concatenate([block_start[1:], jnp.full((1,), total_blocks, jnp.int32)])
    at_shard = jnp.arange(parts, dtype=jnp.int32) == shard_index
    first_block = jnp.sum(jnp.where(at_shard, block_start, 0))
    owned = jnp.sum(jnp.where(at_shard, block_ends - block_start, 0))
    block_index = jnp.arange(total_blocks, dtype=jnp.int32)
    slot_blocks = first_block + jnp.arange(slot_count, dtype=jnp.int32)
    matrix_ids = jnp.sum(
        jnp.where(slot_blocks[:, None] == block_index[None, :], block_matrix[None, :], 0), axis=1
    )
    started = block_start[None, :] <= block_index[:, None]
    owner = jnp.sum(started.astype(jnp.int32), axis=1) - 1
    owner_start = jnp.max(jnp.where(started, block_start[None, :], 0), axis=1)
    slot_of = owner * slot_count + block_index - owner_start
    ints = jnp.concatenate([jnp.stack([owned, (owned - 1) // group]), matrix_ids]).astype(jnp.int32)
    step_value = step[0].astype(jnp.float32)
    beta = 1.0 - step_value ** (-0.8)
    rate = 1.0 / jnp.sqrt(jnp.maximum(step_value, 10000.0))
    floats = jnp.stack([beta, (1.0 - beta) / width, 1.0 - beta, rate])

    smem = pl.BlockSpec(memory_space=pltpu.SMEM)

    def live(i, ints_ref):
        return jnp.minimum(i, ints_ref[1])

    new_rows, sums = pl.pallas_call(
        functools.partial(sums_kernel, group, mats),
        grid_spec=pltpu.PrefetchScalarGridSpec(
            num_scalar_prefetch=1,
            grid=(steps,),
            in_specs=[
                smem,
                pl.BlockSpec((group, height, width), lambda i, s: (live(i, s), 0, 0)),
                pl.BlockSpec((group, height, 1), lambda i, s: (i, 0, 0)),
            ],
            out_specs=[
                pl.BlockSpec((group, height, 1), lambda i, s: (i, 0, 0)),
                pl.BlockSpec((8, width), lambda i, s: (0, 0)),
            ],
            scratch_shapes=[
                pltpu.VMEM((mats, 8, width), jnp.float32),
                pltpu.VMEM((mats, 8, width), jnp.float32),
                pltpu.VMEM((mats, 8, 128), jnp.float32),
            ],
        ),
        out_shape=[
            jax.ShapeDtypeStruct((slot_count, height, 1), jnp.float32),
            jax.ShapeDtypeStruct((8, width), jnp.float32),
        ],
        compiler_params=pltpu.CompilerParams(vmem_limit_bytes=60 * 2**20),
        cost_estimate=pl.CostEstimate(flops=grad.size * 6, bytes_accessed=grad.size * 4, transcendentals=0),
        name="sums",
    )(ints, floats, grad, row_state[:, :, None])

    total = lax.psum(sums, ("shard", "dp"))

    outs = pl.pallas_call(
        functools.partial(update_kernel, group, mats, parts, row_counts),
        grid_spec=pltpu.PrefetchScalarGridSpec(
            num_scalar_prefetch=1,
            grid=(steps,),
            in_specs=[
                smem,
                pl.BlockSpec((group, height, width), lambda i, s: (live(i, s), 0, 0)),
                pl.BlockSpec((group, height, width), lambda i, s: (live(i, s), 0, 0)),
                pl.BlockSpec((group, height, 1), lambda i, s: (live(i, s), 0, 0)),
                pl.BlockSpec((8, width), lambda i, s: (0, 0)),
                pl.BlockSpec((mats, width), lambda i, s: (0, 0)),
            ],
            out_specs=[
                pl.BlockSpec((parts, group, CHUNK, cut), lambda i, s: (0, live(i, s), 0, 0))
                for _ in range(chunks)
            ]
            + [pl.BlockSpec((mats, width), lambda i, s: (0, 0))],
            scratch_shapes=[pltpu.VMEM((mats, 1, width), jnp.float32)],
        ),
        out_shape=[
            jax.ShapeDtypeStruct((parts, slot_count, CHUNK, cut), jnp.bfloat16) for _ in range(chunks)
        ]
        + [jax.ShapeDtypeStruct((mats, width), jnp.float32)],
        compiler_params=pltpu.CompilerParams(vmem_limit_bytes=60 * 2**20),
        cost_estimate=pl.CostEstimate(flops=grad.size * 6, bytes_accessed=grad.size * 8, transcendentals=0),
        name="update",
    )(ints, floats, grad, param, new_rows, total, col_state)
    new_cols = outs[-1]

    dp = lax.axis_size("dp")
    piece_bytes = total_blocks * CHUNK * cut * 2
    placed = None
    run = 12 if total_blocks % 12 == 0 else 1
    for k in range(chunks):
        moved = lax.all_to_all(outs[k], "shard", split_axis=0, concat_axis=0, tiled=True)
        picked = pl.pallas_call(
            pick_kernel,
            in_specs=[smem, pl.BlockSpec(memory_space=pltpu.VMEM)],
            out_specs=pl.BlockSpec(memory_space=pltpu.VMEM),
            out_shape=jax.ShapeDtypeStruct((total_blocks, CHUNK, cut), jnp.bfloat16),
            compiler_params=pltpu.CompilerParams(vmem_limit_bytes=16 * 2**20),
            cost_estimate=pl.CostEstimate(flops=0, bytes_accessed=3 * piece_bytes, transcendentals=0),
            name="pick",
        )(slot_of, moved.reshape(parts * slot_count, CHUNK, cut))
        spread = lax.all_gather(picked, "dp", axis=1, tiled=True)
        spread = spread.reshape(total_blocks, dp, CHUNK, cut)
        old = [] if placed is None else [placed]
        placed = pl.pallas_call(
            place_kernel,
            grid=(total_blocks // run,),
            in_specs=[pl.BlockSpec((run, dp, CHUNK, cut), lambda i: (i, 0, 0, 0))]
            + [pl.BlockSpec(memory_space=pl.ANY) for _ in old],
            out_specs=pl.BlockSpec((run, dp, 1, CHUNK, cut), functools.partial(lambda k, i: (i, 0, k, 0, 0), k)),
            out_shape=jax.ShapeDtypeStruct((total_blocks, dp, chunks, CHUNK, cut), jnp.bfloat16),
            input_output_aliases={1: 0} if old else {},
            compiler_params=pltpu.CompilerParams(vmem_limit_bytes=60 * 2**20),
            cost_estimate=pl.CostEstimate(flops=0, bytes_accessed=2 * dp * piece_bytes, transcendentals=0),
            name="place",
        )(spread, *old)
    new_params = placed.reshape(total_blocks * dp * height, cut)
    return new_params, new_rows[:, :, 0], new_cols


def solution(mesh):
    return jax.shard_map(
        functools.partial(body, mesh.shape["shard"]),
        mesh=mesh,
        in_specs=(
            P("shard", "dp", None),
            P("shard", "dp", None),
            P("shard", "dp"),
            P(),
            P(),
            P(),
            P(),
        ),
        out_specs=(P(None, "shard"), P("shard", "dp"), P()),
        check_vma=False,
    )
```

time: 1280 us -> 583 us (0.46)
  local copies, waits for them, and re-layouts: 345 us -> 3.88 us
  waiting for transfers between devices: 624 us -> 387 us
  blocking collectives: 194 us -> 96.6 us
  other arithmetic: 100 us -> 4.84 us
  Pallas kernels: 0 us -> 61.6 us
    all_gather x1 -> x4, waiting for transfers between devices: 624 us -> 226 us  [body(): spread = lax.all_gather(picked, 'dp', axis=1, tiled=True)]
    unnamed x16 -> x8, local copies, waits for them, and re-layouts: 287 us -> 0.02 us
    psum x0 -> x1, waiting for transfers between devices: none -> 132 us  [body(): total = lax.psum(sums, ('shard', 'dp'))]
    psum x2 -> x0, blocking collectives: 82.8 us -> none  [the longest x1 42.6 us: body(): col_total, row_total = lax.psum((col_part, row_part), ('shard', 'dp'))]
    pallas_call x0 -> x10, Pallas kernels: none -> 61.6 us  [the longest x4 34.3 us: body(): pl.pallas_call(place_kernel, grid=(total_blocks // run,), in_specs=[pl.Bl...]
    unnamed x1 -> x0, other arithmetic: 43.2 us -> none
    all_to_all x1 -> x0, local copies, waits for them, and re-layouts: 38.9 us -> none  [body(): lax.all_to_all(updated, 'shard', split_axis=2, concat_axis=0, tiled=True)]
    reduce_sum x5 -> x3, other arithmetic: 33.4 us -> 2.31 us  [the longest x1 1.37 us: body(): owned = jnp.sum(jnp.where(at_shard, block_ends - block_start, 0))]
  transfers between devices with their start and end apart: 1 -> 6, of which waited for: 1 -> 5; matrix products, arithmetic and copies ran while one was open for 0% -> 0% of each run, Pallas kernels for 0% -> 5%
where the time goes in v1:
time: 583 us; the launch traced here: 582 us
  waiting for transfers between devices  387 us (66%)
  blocking collectives  96.6 us (17%)
  Pallas kernels  61.6 us (11%)
  between operations  15.3 us (3%)
  starting transfers between devices  12.3 us (2%)
    all_gather x4, waiting for transfers between devices, body(): spread = lax.all_gather(picked, 'dp', axis=1, tiled=True)  226 us
    psum x1, waiting for transfers between devices, body(): total = lax.psum(sums, ('shard', 'dp'))  132 us
    all_to_all x3, blocking collectives, body(): lax.all_to_all(outs[k], 'shard', split_axis=0, concat_axis=0, tiled=True)  96.6 us
    pallas_call x4, Pallas kernels, body(): pl.pallas_call(place_kernel, grid=(total_blocks // run,), in_specs=[pl.Bl...  34.3 us
    all_to_all x1, waiting for transfers between devices, body(): lax.all_to_all(outs[k], 'shard', split_axis=0, concat_axis=0, tiled=True)  29.3 us
    all_to_all x1, starting transfers between devices, body(): lax.all_to_all(outs[k], 'shard', split_axis=0, concat_axis=0, tiled=True)  12.1 us
  transfers between devices with their start and end apart: 6, of which 5 were waited for; matrix products, arithmetic and copies ran while one was open for 0% of the time, Pallas kernels for 5%

profile of v1, /device:TPU:0, one launch (start us, length us, event | category | flops | bytes accessed | tf_op | source)
XLA Modules:
  0.0 581.6 jit_solution(10398739230322070936)
XLA Ops:
  7.2 0.0 all-reduce.2.cloned.1.call-start
  7.2 0.7 slice.3
  7.9 1.4 fusion
  10.0 0.7 iota_add_fusion
  11.4 2.1 copy.17.state_ref
  13.5 0.9 select_reduce_fusion
  14.3 0.6 pad_maximum_fusion.floats_ref
  14.9 1.3 pad_add_fusion.ints_ref
  16.2 10.4 %sums.1 = (f32[36,32,1]{2,1,0:T(8,128)}, f32[8,4096]{1,0:T(8,128)}) custom-call(s32[38]{0:T(128)} %pad_add_fusion.ints_ref, f32[4]{0:T(128)} %pad_maximum_fusion.floats_ref, f32[36,32,4096]{2,1,0:T(8,128)} %grad_ref.3, f32[36,32,1]{2,1,0:T(8,128)} %copy.17.state_ref), custom_call_target="tpu_custom_call" | custom-call | flops 28311552 | bytes 18874368 | tf_op jit(solution)/shard_map/sums/pallas_call | solution.py:144
  26.6 0.0 all-reduce.2.cloned.1.call-update
  26.6 132.1 %all-reduce.2.cloned.1.call-done.total_ref = f32[8,4096]{1,0:T(8,128)} async-done(((f32[8,4096]{1,0:T(8,128)}), f32[8,4096]{1,0:T(8,128)}) %all-reduce.2.cloned.1.call-update) | async-done | bytes 131088 | tf_op jit(solution)/shard_map/psum | solution.py:173
  158.7 9.7 %update.1 = (bf16[8,36,8,512]{3,2,1,0:T(8,128)(2,1)}, bf16[8,36,8,512]{3,2,1,0:T(8,128)(2,1)}, bf16[8,36,8,512]{3,2,1,0:T(8,128)(2,1)}, bf16[8,36,8,512]{3,2,1,0:T(8,128)(2,1)}, f32[3,4096]{1,0:T(4,128)}) custom-call(s32[38]{0:T(128)} %pad_add_fusion.ints_ref, f32[4]{0:T(128)} %pad_maximum_fusion.floats_ref, f32[36,32,4096]{2,1,0:T(8,128)} %grad_ref.3, ...), custom_call_target="tpu_custom_call" | custom-call | flops 28311552 | bytes 37748736 | tf_op jit(solution)/shard_map/update/pallas_call | solution.py:175
  168.4 0.0 copy-start.3
  168.4 12.1 %all-to-all-start.3 = ((bf16[8,36,8,512]{3,2,1,0:T(8,128)(2,1)}), bf16[8,36,8,512]{3,2,1,0:T(8,128)(2,1)S(1)}, u32[]{:S(2)}, u32[]{:S(2)}) async-start(bf16[8,36,8,512]{3,2,1,0:T(8,128)(2,1)} %get-tuple-element.15), calls=%async_computation.3 | async-start | bytes 4718592 | tf_op jit(solution)/shard_map/all_to_all | solution.py:210
  180.5 0.0 all-gather.11.cloned.1.call-start
  180.6 0.0 copy-done.3
  180.6 0.1 convert_reduce_fusion
  180.7 29.3 %all-to-all-done.3 = bf16[8,36,8,512]{3,2,1,0:T(8,128)(2,1)S(1)} async-done(((bf16[8,36,8,512]{3,2,1,0:T(8,128)(2,1)}), bf16[8,36,8,512]{3,2,1,0:T(8,128)(2,1)S(1)}, u32[]{:S(2)}, u32[]{:S(2)}) %all-to-all-start.3) | async-done | bytes 2359328 | tf_op jit(solution)/shard_map/all_to_all | solution.py:210
  210.0 1.8 pick.7
  211.8 0.0 all-gather.11.cloned.1.call-update
  211.8 0.0 all-gather.9.cloned.1.call-start
  211.9 32.9 %all_to_all.20 = bf16[8,36,8,512]{3,2,1,0:T(8,128)(2,1)S(1)} all-to-all(bf16[8,36,8,512]{3,2,1,0:T(8,128)(2,1)} %get-tuple-element.14), channel_id=1, replica_groups=mesh['shard'=8,'dp'=4] {'shard'}, dimensions={0} | all-to-all | bytes 4718592 | tf_op jit(solution)/shard_map/all_to_all | solution.py:210
  244.8 0.0 copy-start.1
  244.8 1.8 pick.6
  246.6 0.0 all-gather.9.cloned.1.call-update
  246.6 0.0 all-gather.7.cloned.1.call-start
  246.6 0.0 copy-done.1
  246.7 31.8 %all_to_all.21 = bf16[8,36,8,512]{3,2,1,0:T(8,128)(2,1)S(1)} all-to-all(bf16[8,36,8,512]{3,2,1,0:T(8,128)(2,1)S(1)} %copy-done.1), channel_id=1, replica_groups=mesh['shard'=8,'dp'=4] {'shard'}, dimensions={0} | all-to-all | bytes 4718592 | tf_op jit(solution)/shard_map/all_to_all | solution.py:210
  278.5 0.0 copy-start
  278.5 1.8 pick.5
  280.3 0.0 all-gather.7.cloned.1.call-update
  280.3 0.0 all-gather.5.cloned.1.call-start
  280.4 0.0 copy-done
  280.4 31.8 %all_to_all.22 = bf16[8,36,8,512]{3,2,1,0:T(8,128)(2,1)S(1)} all-to-all(bf16[8,36,8,512]{3,2,1,0:T(8,128)(2,1)S(1)} %copy-done), channel_id=1, replica_groups=mesh['shard'=8,'dp'=4] {'shard'}, dimensions={0} | all-to-all | bytes 4718592 | tf_op jit(solution)/shard_map/all_to_all | solution.py:210
  312.2 0.0 copy-start.2
  312.2 1.9 pick.4
  314.1 0.0 all-gather.5.cloned.1.call-update
  314.1 0.0 copy-done.2
  314.1 1.0 copy.18
  315.1 0.0 all-gather.11.cloned.1.call-done
  315.1 8.5 %place.4.refs_0_ = bf16[144,4,4,8,512]{4,3,2,1,0:T(8,128)(2,1)} custom-call(bf16[144,4,8,512]{3,2,1,0:T(8,128)(2,1)} %bitcast.18), custom_call_target="tpu_custom_call" | custom-call | bytes 9437184 | tf_op jit(solution)/shard_map/place/pallas_call | solution.py:223
  323.7 64.4 %all-gather.9.cloned.1.call-done = bf16[144,32,512]{2,1,0:T(8,128)(2,1)} async-done(((bf16[144,8,512]{2,1,0:T(8,128)(2,1)}), bf16[144,32,512]{2,1,0:T(8,128)(2,1)}) %all-gather.9.cloned.1.call-update) | async-done | bytes 4718608 | tf_op jit(solution)/shard_map/all_gather | solution.py:220
  388.0 8.6 %place.5.refs_0_ = bf16[144,4,4,8,512]{4,3,2,1,0:T(8,128)(2,1)} custom-call(bf16[144,4,8,512]{3,2,1,0:T(8,128)(2,1)} %bitcast.19, bf16[144,4,4,8,512]{4,3,2,1,0:T(8,128)(2,1)} %place.4.refs_0_), custom_call_target="tpu_custom_call", output_to_operand_aliasing={{}: (1, {})} | custom-call | bytes 9437184 | tf_op jit(solution)/shard_map/place/pallas_call | solution.py:223
  396.7 80.6 %all-gather.7.cloned.1.call-done = bf16[144,32,512]{2,1,0:T(8,128)(2,1)} async-done(((bf16[144,8,512]{2,1,0:T(8,128)(2,1)}), bf16[144,32,512]{2,1,0:T(8,128)(2,1)}) %all-gather.7.cloned.1.call-update) | async-done | bytes 4718608 | tf_op jit(solution)/shard_map/all_gather | solution.py:220
  477.3 8.6 %place.6.refs_0_ = bf16[144,4,4,8,512]{4,3,2,1,0:T(8,128)(2,1)} custom-call(bf16[144,4,8,512]{3,2,1,0:T(8,128)(2,1)} %bitcast.20, bf16[144,4,4,8,512]{4,3,2,1,0:T(8,128)(2,1)} %place.5.refs_0_), custom_call_target="tpu_custom_call", output_to_operand_aliasing={{}: (1, {})} | custom-call | bytes 9437184 | tf_op jit(solution)/shard_map/place/pallas_call | solution.py:223
  485.9 80.6 %all-gather.5.cloned.1.call-done = bf16[144,32,512]{2,1,0:T(8,128)(2,1)} async-done(((bf16[144,8,512]{2,1,0:T(8,128)(2,1)}), bf16[144,32,512]{2,1,0:T(8,128)(2,1)}) %all-gather.5.cloned.1.call-update) | async-done | bytes 4718608 | tf_op jit(solution)/shard_map/all_gather | solution.py:220
  566.5 8.5 %place.7 = bf16[144,4,4,8,512]{4,3,2,1,0:T(8,128)(2,1)} custom-call(bf16[144,4,8,512]{3,2,1,0:T(8,128)(2,1)} %bitcast.21, bf16[144,4,4,8,512]{4,3,2,1,0:T(8,128)(2,1)} %place.6.refs_0_), custom_call_target="tpu_custom_call", output_to_operand_aliasing={{}: (1, {})} | custom-call | bytes 9437184 | tf_op jit(solution)/shard_map/place/pallas_call | solution.py:223
  (1 shorter events, 0.0 us)
Async XLA Ops:
  7.2 151.5 %all-reduce.2.cloned.1.call-start = ((), (), s32[]{:S(2)}) async-start(), calls=%async_computation.4 | async-start | bytes 262144 | tf_op jit(solution)/shard_map/psum | solution.py:173
  168.4 12.2 %copy-start.3 = (s32[8]{0:T(128)S(1)}, s32[8]{0:T(128)}, u32[]{:S(2)}) copy-start(s32[8]{0:T(128)} %param.11) | copy-start | bytes 100
  168.4 41.6 %all-to-all-start.3 = ((bf16[8,36,8,512]{3,2,1,0:T(8,128)(2,1)}), bf16[8,36,8,512]{3,2,1,0:T(8,128)(2,1)S(1)}, u32[]{:S(2)}, u32[]{:S(2)}) async-start(bf16[8,36,8,512]{3,2,1,0:T(8,128)(2,1)} %get-tuple-element.15), calls=%async_computation.3 | async-start | bytes 4718592 | tf_op jit(solution)/shard_map/all_to_all | solution.py:210
  180.5 134.6 %all-gather.11.cloned.1.call-start = ((), (), s32[]{:S(2)}) async-start(), calls=%async_computation.8 | async-start | bytes 5898240 | tf_op jit(solution)/shard_map/all_gather | solution.py:220
  211.8 176.2 %all-gather.9.cloned.1.call-start = ((), (), s32[]{:S(2)}) async-start(), calls=%async_computation.7 | async-start | bytes 5898240 | tf_op jit(solution)/shard_map/all_gather | solution.py:220
  244.8 1.9 copy-start.1
  246.6 230.7 %all-gather.7.cloned.1.call-start = ((), (), s32[]{:S(2)}) async-start(), calls=%async_computation.6 | async-start | bytes 5898240 | tf_op jit(solution)/shard_map/all_gather | solution.py:220
  278.5 1.9 copy-start
  280.3 286.2 %all-gather.5.cloned.1.call-start = ((), (), s32[]{:S(2)}) async-start(), calls=%async_computation.5 | async-start | bytes 5898240 | tf_op jit(solution)/shard_map/all_gather | solution.py:220
  312.2 1.9 copy-start.2
Sparse Core Ops, SparseCore 0:
  26.7 131.9 all-reduce.1
  211.9 86.6 all-gather.10
  300.2 87.7 all-gather.8
  389.4 87.7 all-gather.6
  478.7 87.7 all-gather.4

commit v2 on v1

--- a/solution.py
+++ b/solution.py
@@ -17,7 +17,7 @@
     return max(n for n in range(1, 5) if slot_count % n == 0)
 
 
-def sums_kernel(group, mats, ints_ref, floats_ref, grad_ref, state_ref, rows_ref, sums_ref, cols_acc, weighted_acc, rows_acc):
+def sums_kernel(group, mats, piece, ints_ref, floats_ref, grad_ref, state_ref, rows_ref, sums_ref, cols_acc, weighted_acc, rows_acc):
     step = pl.program_id(0)
     owned = ints_ref[0]
     beta = floats_ref[0]
@@ -54,7 +54,9 @@
         for m in range(mats):
             sums_ref[m : m + 1, :] = jnp.sum(cols_acc[m], axis=0, keepdims=True)
             sums_ref[mats + m : mats + m + 1, :] = jnp.sum(weighted_acc[m], axis=0, keepdims=True)
-            sums_ref[2 * mats : 2 * mats + 1, m * 128 : m * 128 + 128] = jnp.sum(rows_acc[m], axis=0, keepdims=True)
+            spot = lax.broadcasted_iota(jnp.int32, (1, sums_ref.shape[1]), 1) % piece == m
+            part = jnp.sum(rows_acc[m], axis=0, keepdims=True)[:, 0:1]
+            sums_ref[2 * mats : 2 * mats + 1, :] += jnp.where(spot, part, 0.0)
 
 
 def update_kernel(group, mats, parts, row_counts, ints_ref, floats_ref, grad_ref, param_ref, rows_ref, total_ref, state_ref, *refs):
@@ -71,7 +73,7 @@
             count = row_counts[m]
             cols = beta * state_ref[m : m + 1, :] + rest * (total_ref[m : m + 1, :] / count)
             cols_ref[m : m + 1, :] = cols
-            average = total_ref[2 * mats : 2 * mats + 1, m * 128 : m * 128 + 1] / count
+            average = total_ref[2 * mats : 2 * mats + 1, m : m + 1] / count
             weighted = total_ref[mats + m : mats + m + 1, :]
             square = average * jnp.sum(weighted / cols, axis=1, keepdims=True)
             clip = jnp.maximum(1.0, jnp.sqrt(square / (count * width)))
@@ -114,6 +116,8 @@
     steps = slot_count // group
     chunks = height // CHUNK
     cut = width // parts
+    every = lax.axis_size(("shard", "dp"))
+    piece = width // every
     row_counts = (float(D), float(D), float(FF))
 
     shard_index = lax.axis_index("shard")
@@ -142,7 +146,7 @@
         return jnp.minimum(i, ints_ref[1])
 
     new_rows, sums = pl.pallas_call(
-        functools.partial(sums_kernel, group, mats),
+        functools.partial(sums_kernel, group, mats, piece),
         grid_spec=pltpu.PrefetchScalarGridSpec(
             num_scalar_prefetch=1,
             grid=(steps,),
@@ -170,7 +174,10 @@
         name="sums",
     )(ints, floats, grad, row_state[:, :, None])
 
-    total = lax.psum(sums, ("shard", "dp"))
+    pieces = sums.reshape(8, every, piece).transpose(1, 0, 2)
+    pieces = lax.all_to_all(pieces, ("shard", "dp"), split_axis=0, concat_axis=0, tiled=True)
+    total = lax.all_gather(jnp.sum(pieces, axis=0), ("shard", "dp"), axis=0)
+    total = total.transpose(1, 0, 2).reshape(8, width)
 
     outs = pl.pallas_call(
         functools.partial(update_kernel, group, mats, parts, row_counts),

time: 583 us -> 539 us (0.925)
  waiting for transfers between devices: 387 us -> 255 us
  blocking collectives: 96.6 us -> 190 us
  Pallas kernels: 61.6 us -> 54.4 us
    psum x1 -> x0, waiting for transfers between devices: 132 us -> none  [body(): total = lax.psum(sums, ('shard', 'dp'))]
    all_gather x0 -> x1, blocking collectives: none -> 69.9 us  [body(): total = lax.all_gather(jnp.sum(pieces, axis=0), ('shard', 'dp'), axis=0)]
    all_to_all x0 -> x1, blocking collectives: none -> 23.4 us  [body(): lax.all_to_all(pieces, ('shard', 'dp'), split_axis=0, concat_axis=0, tile...]
  transfers between devices with their start and end apart: 6 -> 5, of which waited for: 5 -> 4; matrix products, arithmetic and copies ran while one was open for 0% -> 0% of each run, Pallas kernels for 5% -> 6%
where the time goes in v2:
time: 539 us
  waiting for transfers between devices  255 us (47%)
  blocking collectives  190 us (35%)
  Pallas kernels  54.4 us (10%)
  starting transfers between devices  15.8 us (3%)
  between operations  15.2 us (3%)
    all_gather x4, waiting for transfers between devices, body(): spread = lax.all_gather(picked, 'dp', axis=1, tiled=True)  225 us
    all_to_all x3, blocking collectives, body(): lax.all_to_all(outs[k], 'shard', split_axis=0, concat_axis=0, tiled=True)  96.6 us
    all_gather x1, blocking collectives, body(): total = lax.all_gather(jnp.sum(pieces, axis=0), ('shard', 'dp'), axis=0)  69.9 us
    pallas_call x4, Pallas kernels, body(): pl.pallas_call(place_kernel, grid=(total_blocks // run,), in_specs=[pl.Bl...  34.3 us
    all_to_all x1, waiting for transfers between devices, body(): lax.all_to_all(outs[k], 'shard', split_axis=0, concat_axis=0, tiled=True)  29.3 us
    all_to_all x1, blocking collectives, body(): lax.all_to_all(pieces, ('shard', 'dp'), split_axis=0, concat_axis=0, tile...  23.4 us
    all_to_all x1, starting transfers between devices, body(): lax.all_to_all(outs[k], 'shard', split_axis=0, concat_axis=0, tiled=True)  15.6 us
  transfers between devices with their start and end apart: 5, of which 4 were waited for; matrix products, arithmetic and copies ran while one was open for 0% of the time, Pallas kernels for 6%

profile of v2, /device:TPU:0, one launch (start us, length us, event | category | flops | bytes accessed | tf_op | source)
XLA Modules:
  0.0 538.6 jit_solution(6129296501298714419)
XLA Ops:
  7.2 0.7 slice.3
  7.9 1.4 fusion
  9.9 0.7 iota_add_fusion
  11.3 2.1 copy.17.state_ref
  13.4 0.9 select_reduce_fusion
  14.3 0.6 pad_maximum_fusion.floats_ref
  14.9 1.3 pad_add_fusion.ints_ref
  16.2 7.6 %sums.1 = (f32[36,32,1]{2,1,0:T(8,128)}, f32[8,4096]{1,0:T(8,128)}) custom-call(s32[38]{0:T(128)} %pad_add_fusion.ints_ref, f32[4]{0:T(128)} %pad_maximum_fusion.floats_ref, f32[36,32,4096]{2,1,0:T(8,128)} %grad_ref.3, f32[36,32,1]{2,1,0:T(8,128)} %copy.17.state_ref), custom_call_target="tpu_custom_call" | custom-call | flops 28311552 | bytes 18874368 | tf_op jit(solution)/shard_map/sums/pallas_call | solution.py:148
  23.8 23.4 %all_to_all.25 = f32[32,8,128]{2,1,0:T(8,128)S(1)} all-to-all(f32[32,8,128]{2,1,0:T(8,128)} %bitcast.31), channel_id=1, replica_groups=mesh['shard'=8,'dp'=4] {'shard','dp'}, dimensions={0} | all-to-all | bytes 262144 | tf_op jit(solution)/shard_map/all_to_all | solution.py:178
  47.2 69.9 %all-gather = f32[256,128]{1,0:T(8,128)} all-gather(f32[8,128]{1,0:T(8,128)S(1)} %reduce_sum.49), channel_id=2, replica_groups=mesh['shard'=8,'dp'=4] {'shard','dp'}, dimensions={0}, use_global_device_ids=true | all-gather | bytes 135168 | tf_op jit(solution)/shard_map/all_gather | solution.py:179
  117.1 5.2 update.1
  122.3 0.0 copy-start.3
  122.3 15.6 %all-to-all-start.4 = ((bf16[8,36,8,512]{3,2,1,0:T(8,128)(2,1)}), bf16[8,36,8,512]{3,2,1,0:T(8,128)(2,1)S(1)}, u32[]{:S(2)}, u32[]{:S(2)}) async-start(bf16[8,36,8,512]{3,2,1,0:T(8,128)(2,1)} %get-tuple-element.15), calls=%async_computation.4 | async-start | bytes 4718592 | tf_op jit(solution)/shard_map/all_to_all | solution.py:217
  137.9 0.0 all-gather.12.cloned.1.call-start
  138.0 0.0 copy-done.3
  138.0 0.1 convert_reduce_fusion
  138.1 29.3 %all-to-all-done.4 = bf16[8,36,8,512]{3,2,1,0:T(8,128)(2,1)S(1)} async-done(((bf16[8,36,8,512]{3,2,1,0:T(8,128)(2,1)}), bf16[8,36,8,512]{3,2,1,0:T(8,128)(2,1)S(1)}, u32[]{:S(2)}, u32[]{:S(2)}) %all-to-all-start.4) | async-done | bytes 2359328 | tf_op jit(solution)/shard_map/all_to_all | solution.py:217
  167.4 1.8 pick.7
  169.2 0.0 all-gather.12.cloned.1.call-update
  169.2 0.0 all-gather.10.cloned.1.call-start
  169.2 32.9 %all_to_all.26 = bf16[8,36,8,512]{3,2,1,0:T(8,128)(2,1)S(1)} all-to-all(bf16[8,36,8,512]{3,2,1,0:T(8,128)(2,1)} %get-tuple-element.14), channel_id=1, replica_groups=mesh['shard'=8,'dp'=4] {'shard'}, dimensions={0} | all-to-all | bytes 4718592 | tf_op jit(solution)/shard_map/all_to_all | solution.py:217
  202.1 0.0 copy-start.1
  202.1 1.8 pick.6
  204.0 0.0 all-gather.10.cloned.1.call-update
  204.0 0.0 all-gather.8.cloned.1.call-start
  204.1 0.0 copy-done.1
  204.1 31.8 %all_to_all.27 = bf16[8,36,8,512]{3,2,1,0:T(8,128)(2,1)S(1)} all-to-all(bf16[8,36,8,512]{3,2,1,0:T(8,128)(2,1)S(1)} %copy-done.1), channel_id=1, replica_groups=mesh['shard'=8,'dp'=4] {'shard'}, dimensions={0} | all-to-all | bytes 4718592 | tf_op jit(solution)/shard_map/all_to_all | solution.py:217
  235.9 0.0 copy-start
  235.9 1.8 pick.5
  237.7 0.0 all-gather.8.cloned.1.call-update
  237.7 0.0 all-gather.6.cloned.1.call-start
  237.8 0.0 copy-done
  237.8 31.8 %all_to_all.28 = bf16[8,36,8,512]{3,2,1,0:T(8,128)(2,1)S(1)} all-to-all(bf16[8,36,8,512]{3,2,1,0:T(8,128)(2,1)S(1)} %copy-done), channel_id=1, replica_groups=mesh['shard'=8,'dp'=4] {'shard'}, dimensions={0} | all-to-all | bytes 4718592 | tf_op jit(solution)/shard_map/all_to_all | solution.py:217
  269.6 0.0 copy-start.2
  269.6 1.9 pick.4
  271.5 0.0 all-gather.6.cloned.1.call-update
  271.5 0.0 copy-done.2
  271.5 1.0 copy.18
  272.6 0.0 all-gather.12.cloned.1.call-done
  272.6 8.5 %place.4.refs_0_ = bf16[144,4,4,8,512]{4,3,2,1,0:T(8,128)(2,1)} custom-call(bf16[144,4,8,512]{3,2,1,0:T(8,128)(2,1)} %bitcast.26), custom_call_target="tpu_custom_call" | custom-call | bytes 9437184 | tf_op jit(solution)/shard_map/place/pallas_call | solution.py:230
  281.1 63.8 %all-gather.10.cloned.1.call-done = bf16[144,32,512]{2,1,0:T(8,128)(2,1)} async-done(((bf16[144,8,512]{2,1,0:T(8,128)(2,1)}), bf16[144,32,512]{2,1,0:T(8,128)(2,1)}) %all-gather.10.cloned.1.call-update) | async-done | bytes 4718608 | tf_op jit(solution)/shard_map/all_gather | solution.py:227
  344.9 8.6 %place.5.refs_0_ = bf16[144,4,4,8,512]{4,3,2,1,0:T(8,128)(2,1)} custom-call(bf16[144,4,8,512]{3,2,1,0:T(8,128)(2,1)} %bitcast.27, bf16[144,4,4,8,512]{4,3,2,1,0:T(8,128)(2,1)} %place.4.refs_0_), custom_call_target="tpu_custom_call", output_to_operand_aliasing={{}: (1, {})} | custom-call | bytes 9437184 | tf_op jit(solution)/shard_map/place/pallas_call | solution.py:230
  353.5 80.8 %all-gather.8.cloned.1.call-done = bf16[144,32,512]{2,1,0:T(8,128)(2,1)} async-done(((bf16[144,8,512]{2,1,0:T(8,128)(2,1)}), bf16[144,32,512]{2,1,0:T(8,128)(2,1)}) %all-gather.8.cloned.1.call-update) | async-done | bytes 4718608 | tf_op jit(solution)/shard_map/all_gather | solution.py:227
  434.3 8.6 %place.6.refs_0_ = bf16[144,4,4,8,512]{4,3,2,1,0:T(8,128)(2,1)} custom-call(bf16[144,4,8,512]{3,2,1,0:T(8,128)(2,1)} %bitcast.28, bf16[144,4,4,8,512]{4,3,2,1,0:T(8,128)(2,1)} %place.5.refs_0_), custom_call_target="tpu_custom_call", output_to_operand_aliasing={{}: (1, {})} | custom-call | bytes 9437184 | tf_op jit(solution)/shard_map/place/pallas_call | solution.py:230
  442.9 80.6 %all-gather.6.cloned.1.call-done = bf16[144,32,512]{2,1,0:T(8,128)(2,1)} async-done(((bf16[144,8,512]{2,1,0:T(8,128)(2,1)}), bf16[144,32,512]{2,1,0:T(8,128)(2,1)}) %all-gather.6.cloned.1.call-update) | async-done | bytes 4718608 | tf_op jit(solution)/shard_map/all_gather | solution.py:227
  523.5 8.5 %place.7 = bf16[144,4,4,8,512]{4,3,2,1,0:T(8,128)(2,1)} custom-call(bf16[144,4,8,512]{3,2,1,0:T(8,128)(2,1)} %bitcast.29, bf16[144,4,4,8,512]{4,3,2,1,0:T(8,128)(2,1)} %place.6.refs_0_), custom_call_target="tpu_custom_call", output_to_operand_aliasing={{}: (1, {})} | custom-call | bytes 9437184 | tf_op jit(solution)/shard_map/place/pallas_call | solution.py:230
  (2 shorter events, 0.0 us)
Async XLA Ops:
  122.3 15.7 %copy-start.3 = (s32[8]{0:T(128)S(1)}, s32[8]{0:T(128)}, u32[]{:S(2)}) copy-start(s32[8]{0:T(128)} %param.11) | copy-start | bytes 100
  122.3 45.0 %all-to-all-start.4 = ((bf16[8,36,8,512]{3,2,1,0:T(8,128)(2,1)}), bf16[8,36,8,512]{3,2,1,0:T(8,128)(2,1)S(1)}, u32[]{:S(2)}, u32[]{:S(2)}) async-start(bf16[8,36,8,512]{3,2,1,0:T(8,128)(2,1)} %get-tuple-element.15), calls=%async_computation.4 | async-start | bytes 4718592 | tf_op jit(solution)/shard_map/all_to_all | solution.py:217
  137.9 134.6 %all-gather.12.cloned.1.call-start = ((), (), s32[]{:S(2)}) async-start(), calls=%async_computation.8 | async-start | bytes 5898240 | tf_op jit(solution)/shard_map/all_gather | solution.py:227
  169.2 175.7 %all-gather.10.cloned.1.call-start = ((), (), s32[]{:S(2)}) async-start(), calls=%async_computation.7 | async-start | bytes 5898240 | tf_op jit(solution)/shard_map/all_gather | solution.py:227
  202.1 1.9 copy-start.1
  204.0 230.3 %all-gather.8.cloned.1.call-start = ((), (), s32[]{:S(2)}) async-start(), calls=%async_computation.6 | async-start | bytes 5898240 | tf_op jit(solution)/shard_map/all_gather | solution.py:227
  235.9 1.9 copy-start
  237.7 285.8 %all-gather.6.cloned.1.call-start = ((), (), s32[]{:S(2)}) async-start(), calls=%async_computation.5 | async-start | bytes 5898240 | tf_op jit(solution)/shard_map/all_gather | solution.py:227
  269.6 1.9 copy-start.2
Sparse Core Ops, SparseCore 0:
  169.3 86.1 all-gather.11
  257.0 87.7 all-gather.9
  346.4 87.7 all-gather.7
  435.7 87.7 all-gather.5
